TPU v7x, 128 devices: a whole 4x4x4 slice. The times are simulated.
128 devices in a mesh: ga: 128 (over z, y, x, core).
Axes of the slice: x: 4, y: 4, z: 4, core: 2. Of those that a mesh axis runs over, the one named last changes fastest.
Arguments:
- text_states: bfloat16 [2048, 640], P('ga')
- text_proj: bfloat16 [640, 640], replicated
- gallery: bfloat16 [262144, 640], P('ga')
- logit_scale: float32 [1], replicated
Outputs:
- output 1: bfloat16 [2048, 262144], P(None, 'ga')
- output 2: float32 [2048], replicated
All inputs are finite; a program needn't handle non-finite values.
Results may differ from a plain program's by a relative error of at most 0.001.
Values are sent between devices in bfloat16 or wider.
A program may use at most 1 GiB of HBM per device.

v0:
```python
import jax
import jax.numpy as jnp
from jax import lax
from jax.sharding import PartitionSpec as P, NamedSharding


def solution(mesh):
    num_dev = mesh.shape["ga"]

    def per_device(text_states, text_proj, gallery, logit_scale):
        proj_out = jnp.dot(text_states, text_proj, preferred_element_type=jnp.float32)
        unit_q = proj_out / jnp.sqrt(jnp.sum(proj_out * proj_out, axis=1, keepdims=True))
        query_emb = unit_q.astype(jnp.bfloat16)
        all_queries = lax.all_gather(query_emb, "ga", axis=0, tiled=True)
        logit_mult = jnp.exp(logit_scale[0])
        scores = logit_mult * lax.dot_general(all_queries, gallery, (((1,), (1,)), ((), ())),
                                              preferred_element_type=jnp.float32)
        glob_max = lax.pmax(jnp.max(scores, axis=1), "ga")
        exp_vals = jnp.exp(scores - glob_max[:, None])
        glob_sum = lax.psum(jnp.sum(exp_vals, axis=1), "ga")
        prob_vals = exp_vals / glob_sum[:, None]
        local_rows = gallery.shape[0]
        total_rows = local_rows * num_dev
        row_ids = lax.axis_index("ga") * local_rows + jnp.arange(local_rows, dtype=jnp.int32)
        positions = row_ids.astype(jnp.float32) / total_rows
        exp_rank = lax.psum(jnp.sum(prob_vals * positions, axis=1), "ga")
        return prob_vals.astype(jnp.bfloat16), exp_rank

    return jax.shard_map(per_device, mesh=mesh,
                         in_specs=(P("ga", None), P(None, None), P("ga", None), P(None)),
                         out_specs=(P(None, "ga"), P(None)), check_vma=False)
```

profile of v0, /device:TPU:1, one launch (start us, length us, event | category | flops | bytes accessed | tf_op | source)
XLA Modules:
  0.0 319.2 jit_solution(6264593759662458142)
XLA Ops:
  7.2 0.0 copy-start
  7.2 0.0 all-gather.2.cloned.1.call-start
  7.2 1.6 multiply_reduce_fusion.2
  8.9 0.7 divide_convert_fusion
  9.6 0.0 all-gather.2.cloned.1.call-update
  10.3 70.4 %all-gather.2.cloned.1.call-done = bf16[2048,640]{1,0:T(8,128)(2,1)} async-done(((bf16[16,640]{1,0:T(8,128)(2,1)}), bf16[2048,640]{1,0:T(8,128)(2,1)}) %all-gather.2.cloned.1.call-update) | async-done | bytes 2621456 | tf_op jit(solution)/shard_map/all_gather | solution.py:14
  80.7 0.0 copy-done
  80.8 11.3 %multiply_reduce_fusion.1 = (f32[2048]{0:T(1024)S(1)}, f32[2048,2048]{0,1:T(8,128)}) fusion(f32[]{:T(128)} %bitcast, bf16[2048,640]{1,0:T(8,128)(2,1)} %all-gather.2.cloned.1.call-done, bf16[2048,640]{1,0:T(8,128)(2,1)S(1)} %copy-done), kind=kOutput, calls=%fused_computation.2 | convolution fusion | flops 5377095680 | bytes 22028292 | tf_op jit(solution)/shard_map/dot_general | solution.py:16
  92.1 62.3 %pmax.7 = f32[2048]{0:T(1024)S(1)} all-reduce(f32[2048]{0:T(1024)S(1)} %get-tuple-element.8), channel_id=1, replica_groups=mesh['ga'=128] {'ga'}, use_global_device_ids=true, to_apply=%region_2.0 | all-reduce | flops 2048 | bytes 16384 | tf_op jit(solution)/shard_map/pmax | solution.py:18
  154.4 8.5 %fusion.1 = f32[2048]{0:T(1024)S(1)} fusion(f32[2048,2048]{0,1:T(8,128)} %get-tuple-element.9, f32[2048]{0:T(1024)S(1)} %pmax.7, f32[]{:T(128)} %bitcast), kind=kLoop, calls=%fused_computation.4 | loop fusion | flops 12580864 | bytes 16793604 | tf_op jit(solution)/shard_map/reduce_sum | solution.py:20
  163.0 63.8 %psum.14 = f32[2048]{0:T(1024)S(1)} all-reduce(f32[2048]{0:T(1024)S(1)} %fusion.1), channel_id=1, replica_groups=mesh['ga'=128] {'ga'}, use_global_device_ids=true, to_apply=%region_4.0 | all-reduce | flops 2048 | bytes 16384 | tf_op jit(solution)/shard_map/psum | solution.py:20
  226.8 10.9 %multiply_reduce_fusion = (f32[2048]{0:T(1024)S(1)}, bf16[2048,2048]{0,1:T(8,128)(2,1)}) fusion(f32[2048]{0:T(1024)S(1)} %convert_multiply_fusion, f32[2048]{0:T(1024)S(1)} %psum.14, f32[2048]{0:T(1024)S(1)} %pmax.7, f32[2048,2048]{0,1:T(8,128)} %get-tuple-element.9, f32[]{:T(128)} %bitcast), kind=kLoop, calls=%fused_computation | loop fusion | flops 25163776 | bytes 25198596 | tf_op jit(solution)/shard_map/reduce_sum | solution.py:26
  237.6 62.5 %psum.15 = f32[2048]{0:T(1024)} all-reduce(f32[2048]{0:T(1024)S(1)} %get-tuple-element.4), channel_id=1, replica_groups=mesh['ga'=128] {'ga'}, use_global_device_ids=true, to_apply=%region_6.0 | all-reduce | flops 2048 | bytes 16384 | tf_op jit(solution)/shard_map/psum | solution.py:26
  300.1 12.2 %copy.6 = bf16[2048,2048]{1,0:T(8,128)(2,1)} copy(bf16[2048,2048]{0,1:T(8,128)(2,1)} %get-tuple-element.5) | data formatting | bytes 16777216
  (2 shorter events, 0.0 us)
Async XLA Ops:
  7.2 73.6 %copy-start = (bf16[2048,640]{1,0:T(8,128)(2,1)S(1)}, bf16[2048,640]{1,0:T(8,128)(2,1)}, u32[]{:S(2)}) copy-start(bf16[2048,640]{1,0:T(8,128)(2,1)} %param.6) | copy-start | bytes 7864324
  7.2 73.6 %all-gather.2.cloned.1.call-start = ((), (), s32[]{:S(2)}) async-start(), calls=%async_computation | async-start | bytes 2641920 | tf_op jit(solution)/shard_map/all_gather | solution.py:14
Sparse Core Ops, SparseCore 0:
  11.7 69.0 all-gather.1
where the time goes:
time: 320 us; the launch traced here: 319 us
  blocking collectives  189 us (59%)
  waiting for transfers between devices  70.4 us (22%)
  other arithmetic  20.1 us (6%)
  between operations  14.7 us (5%)
  matrix products  13 us (4%)
  local copies, waits for them, and re-layouts  12.2 us (4%)
    all_gather x1, waiting for transfers between devices, per_device(): all_queries = lax.all_gather(query_emb, 'ga', axis=0, tiled=True)  70.4 us
    psum x1, blocking collectives, per_device(): glob_sum = lax.psum(jnp.sum(exp_vals, axis=1), 'ga')  63.8 us
    psum x1, blocking collectives, per_device(): exp_rank = lax.psum(jnp.sum(prob_vals * positions, axis=1), 'ga')  62.5 us
    pmax x1, blocking collectives, per_device(): glob_max = lax.pmax(jnp.max(scores, axis=1), 'ga')  62.3 us
    unnamed x3, local copies, waits for them, and re-layouts  12.2 us
    dot_general x1, matrix products, per_device(): lax.dot_general(all_queries, gallery, (((1,), (1,)), ((), ())), preferred...  11.3 us
    reduce_sum x1, other arithmetic, per_device(): exp_rank = lax.psum(jnp.sum(prob_vals * positions, axis=1), 'ga')  10.9 us
    reduce_sum x1, other arithmetic, per_device(): glob_sum = lax.psum(jnp.sum(exp_vals, axis=1), 'ga')  8.55 us
  transfers between devices with their start and end apart: 1, of which 1 were waited for; matrix products, arithmetic and copies ran while one was open for 0% of the time, Pallas kernels for 0%

commit v1 on v0

v1 whole, which is shorter than its diff:
```python
import jax
import jax.numpy as jnp
from jax import lax
from jax.experimental import pallas as pl
from jax.experimental.pallas import tpu as pltpu
from jax.sharding import PartitionSpec as P

MESH = pl.DeviceIdType.MESH
LOG2E = 1.4426950408889634
Z, Y, X = 0, 1, 2
ROUTES = (((X, Y, Z), 0, 256), ((Y, Z, X), 256, 256), ((Z, X, Y), 512, 128))
CHUNK = 256


def device_of(pos, core):
    return ((pos[0] * 4 + pos[1]) * 4 + pos[2]) * 2 + core


def kernel(t_hbm, w_hbm, g_hbm, scale_ref, p_ref, rank_ref,
           t_buf, w_buf, g_buf, q_all, e_buf, max_buf, sum_buf, pos_buf, stat_own, stat_in,
           load_sem, gs_sem, gr_sem, ss_sem, sr_sem):
    me = lax.axis_index("ga")
    core = lax.rem(me, 2)
    pos = (me // 32, lax.rem(me // 8, 4), lax.rem(me // 2, 4))
    partner = me + 1 - 2 * core

    def peer(axis, k):
        there = list(pos)
        there[axis] = lax.rem(pos[axis] + k, 4)
        return device_of(there, core)

    loads = [pltpu.make_async_copy(src, dst, load_sem.at[i])
             for i, (src, dst) in enumerate(((t_hbm, t_buf), (w_hbm, w_buf), (g_hbm, g_buf)))]
    for load in loads:
        load.start()
    barrier = pltpu.get_barrier_semaphore()
    pl.semaphore_signal(barrier, inc=1, device_id=(partner,), device_id_type=MESH)
    for axis in range(3):
        for k in range(1, 4):
            pl.semaphore_signal(barrier, inc=1, device_id=(peer(axis, k),), device_id_type=MESH)

    mult = jnp.exp(jnp.full((1, 128), scale_ref[0], jnp.float32))
    coef = mult * (LOG2E / 2)

    loads[0].wait()
    loads[1].wait()
    u = jnp.dot(t_buf[...], w_buf[...], preferred_element_type=jnp.float32)
    unit = u / jnp.sqrt(jnp.sum(u * u, axis=1, keepdims=True))
    q_all[pos[0], pos[1], pos[2], core] = (unit * 2.0).astype(jnp.bfloat16)
    pl.semaphore_wait(barrier, 10)

    sends = []
    counter = [0]

    def view(fixed, c, col, ncol):
        idx = tuple(fixed[a] if a in fixed else slice(None) for a in range(3))
        return q_all.at[idx + (c, slice(None), pl.ds(col, ncol))]

    def send(fixed, col, ncol, slot, to):
        ref = view(fixed, core, col, ncol)
        copy = pltpu.make_async_remote_copy(ref, ref, gs_sem.at[slot], gr_sem.at[slot],
                                            device_id=(to,), device_id_type=MESH)
        copy.start()
        sends.append(copy)

    def recv(fixed, c, col, ncol, slot):
        ref = view(fixed, c, col, ncol)
        pltpu.make_async_remote_copy(ref, ref, gs_sem.at[slot], gr_sem.at[slot],
                                     device_id=(partner,), device_id_type=MESH).wait_recv()

    def fixed_at(order, phase, k=0):
        out = {}
        for i in range(phase, 3):
            a = order[i]
            out[a] = lax.rem(pos[a] + 4 - k, 4) if i == phase else pos[a]
        return out

    cross = []
    for phase in range(3):
        for r, (order, col, ncol) in enumerate(ROUTES):
            if phase > 0:
                for k in range(1, 4):
                    recv(fixed_at(order, phase - 1, k), core, col, ncol, r * 16 + (phase - 1) * 3 + k - 1)
            fixed = fixed_at(order, phase)
            for k in range(1, 4):
                send(fixed, col, ncol, r * 16 + phase * 3 + k - 1, peer(order[phase], k))
            if phase == 2:
                send(fixed, col, ncol, r * 16 + 9, partner)
                cross.append((fixed, col, ncol, r * 16 + 9))
    for k in range(1, 4):
        for r, (order, col, ncol) in enumerate(ROUTES):
            fixed = fixed_at(order, 2, k)
            recv(fixed, core, col, ncol, r * 16 + 6 + k - 1)
            send(fixed, col, ncol, r * 16 + 9 + k, partner)
            cross.append((fixed, col, ncol, r * 16 + 9 + k))
    for fixed, col, ncol, slot in cross:
        recv(fixed, 1 - core, col, ncol, slot)

    loads[2].wait()

    @pl.loop(0, 2048 // CHUNK)
    def _(i):
        rows = pl.multiple_of(i * CHUNK, CHUNK)
        q = q_all[i // 2, pl.ds(lax.rem(i, 2) * 2, 2)].reshape(CHUNK, 640)
        for n in range(8):
            e_buf[pl.ds(rows, CHUNK), n * 256:(n + 1) * 256] = lax.dot_general(
                q, g_buf[n * 256:(n + 1) * 256, :], (((1,), (1,)), ((), ())),
                preferred_element_type=jnp.float32)

        @pl.loop(0, CHUNK // 8, unroll=4)
        def _(j):
            r8 = pl.ds(pl.multiple_of(rows + j * 8, 8), 8)
            d = [e_buf[r8, c * 128:(c + 1) * 128] for c in range(16)]
            top = d
            while len(top) > 1:
                top = [jnp.maximum(a, b) for a, b in zip(top[::2], top[1::2])]
            top = top[0]
            total = None
            for c in range(15, -1, -1):
                e = jnp.exp2((d[c] - top) * coef)
                e_buf[r8, c * 128:(c + 1) * 128] = e
                total = e if total is None else total + e
                if c == 15:
                    weighted = total
                elif c > 0:
                    weighted = weighted + total
            max_buf[r8, :] = top
            sum_buf[r8, :] = total
            pos_buf[r8, :] = weighted

    base = (me * 2048).astype(jnp.float32)
    lane = lax.broadcasted_iota(jnp.int32, (128, 128), 0).astype(jnp.float32) + base

    @pl.loop(0, 16)
    def _(b):
        r128 = pl.ds(pl.multiple_of(b * 128, 128), 128)
        m_t = max_buf[r128, :].T
        z_t = sum_buf[r128, :].T
        w_t = pos_buf[r128, :].T
        m = jnp.max(m_t, axis=0, keepdims=True)
        scale = jnp.exp2((m_t - m) * coef)
        max_buf[r128, :] = m_t
        stat_own[0, pl.ds(b, 1), :] = m
        stat_own[1, pl.ds(b, 1), :] = jnp.sum(z_t * scale, axis=0, keepdims=True)
        stat_own[2, pl.ds(b, 1), :] = jnp.sum((z_t * lane + w_t * 128.0) * scale, axis=0, keepdims=True)

    def merge(parts):
        m = parts[0][0]
        for part in parts[1:]:
            m = jnp.maximum(m, part[0])
        z = s = None
        for pm, pz, ps in parts:
            f = jnp.exp2((pm - m) * coef)
            z = pz * f if z is None else z + pz * f
            s = ps * f if s is None else s + ps * f
        return m, z, s

    stage_axes = (None, X, Y, Z)
    for stage, axis in enumerate(stage_axes):
        if axis is None:
            here, others, n = core, [(partner, 0)], 2
        else:
            here, others, n = pos[axis], [(peer(axis, k), k - 1) for k in range(1, 4)], 4
        slots = stat_in.at[stage]
        slots[here] = stat_own[...]
        copies = []
        for to, k in others:
            copy = pltpu.make_async_remote_copy(
                stat_in.at[stage, here], stat_in.at[stage, here], ss_sem.at[stage, k], sr_sem.at[stage, k],
                device_id=(to,), device_id_type=MESH)
            copy.start()
            copies.append(copy)
            sends.append(copy)
        for copy in copies:
            copy.wait_recv()
        m, z, s = merge([tuple(slots[a, i] for i in range(3)) for a in range(n)])
        stat_own[0] = m
        stat_own[1] = z
        stat_own[2] = s
    rank_ref[...] = s / (z * 262144.0)

    @pl.loop(0, 16)
    def _(b):
        r128 = pl.ds(pl.multiple_of(b * 128, 128), 128)
        m = stat_own[0, pl.ds(b, 1), :]
        z = stat_own[1, pl.ds(b, 1), :]
        sum_buf[r128, :] = (jnp.exp2((max_buf[r128, :] - m) * coef) / z).T

    @pl.loop(0, 128, unroll=2)
    def _(j):
        r16 = pl.ds(pl.multiple_of(j * 16, 16), 16)
        f = sum_buf[r16, :]
        for c in range(16):
            p_ref[r16, c * 128:(c + 1) * 128] = (e_buf[r16, c * 128:(c + 1) * 128] * f).astype(jnp.bfloat16)

    for copy in sends:
        copy.wait_send()


def solution(mesh):
    def per_device(text_states, text_proj, gallery, logit_scale):
        p, rank = pl.pallas_call(
            kernel,
            out_shape=[pltpu.VMEM((2048, 2048), jnp.bfloat16), pltpu.VMEM((16, 128), jnp.float32)],
            in_specs=[pl.BlockSpec(memory_space=pltpu.HBM)] * 3 + [pl.BlockSpec(memory_space=pltpu.SMEM)],
            out_specs=[pl.BlockSpec(memory_space=pltpu.VMEM)] * 2,
            scratch_shapes=[
                pltpu.VMEM((16, 640), jnp.bfloat16),
                pltpu.VMEM((640, 640), jnp.bfloat16),
                pltpu.VMEM((2048, 640), jnp.bfloat16),
                pltpu.VMEM((4, 4, 4, 2, 16, 640), jnp.bfloat16),
                pltpu.VMEM((2048, 2048), jnp.float32),
                pltpu.VMEM((2048, 128), jnp.float32),
                pltpu.VMEM((2048, 128), jnp.float32),
                pltpu.VMEM((2048, 128), jnp.float32),
                pltpu.VMEM((3, 16, 128), jnp.float32),
                pltpu.VMEM((4, 4, 3, 16, 128), jnp.float32),
                pltpu.SemaphoreType.DMA((3,)),
                pltpu.SemaphoreType.DMA((48,)),
                pltpu.SemaphoreType.DMA((48,)),
                pltpu.SemaphoreType.DMA((4, 3)),
                pltpu.SemaphoreType.DMA((4, 3)),
            ],
            compiler_params=pltpu.CompilerParams(
                collective_id=0, has_side_effects=True, vmem_limit_bytes=40 * 2**20),
        )(text_states, text_proj, gallery, logit_scale)
        return p, rank.reshape(2048)

    return jax.shard_map(per_device, mesh=mesh,
                         in_specs=(P("ga", None), P(None, None), P("ga", None), P(None)),
                         out_specs=(P(None, "ga"), P(None)), check_vma=False)
```

time: 320 us -> 67.1 us (0.21)
  the two profiles are of different devices: /device:TPU:1 before, /device:TPU:0 now
where the time goes in v1:
time: 67.1 us; the launch traced here: 66.8 us
  Pallas kernels  57.9 us (86%)
  local copies, waits for them, and re-layouts  7.6 us (11%)
  between operations  1.3 us (2%)
    pallas_call x1, Pallas kernels, per_device(): pl.pallas_call(kernel, out_shape=[pltpu.VMEM((2048, 2048), jnp.bfloat16),...  57.9 us
    unnamed x8, local copies, waits for them, and re-layouts  7.6 us

profile of v1, /device:TPU:0, one launch (start us, length us, event | category | flops | bytes accessed | tf_op | source)
XLA Modules:
  0.0 66.8 jit_solution(6525037528535457243)
XLA Ops:
  1.3 0.0 copy-start
  1.3 1.7 %copy-done = bf16[2048,640]{1,0:T(8,128)(2,1)S(1)} copy-done((bf16[2048,640]{1,0:T(8,128)(2,1)S(1)}, bf16[2048,640]{1,0:T(8,128)(2,1)}, u32[]{:S(2)}) %copy-start) | copy-done | bytes 2621464
  3.0 0.0 copy-start.1
  3.0 1.1 %copy-done.1 = bf16[640,640]{1,0:T(8,128)(2,1)S(1)} copy-done((bf16[640,640]{1,0:T(8,128)(2,1)S(1)}, bf16[640,640]{1,0:T(8,128)(2,1)}, u32[]{:S(2)}) %copy-start.1) | copy-done | bytes 819224
  4.2 0.0 copy-start.2
  4.2 0.7 %copy-done.2 = bf16[16,640]{1,0:T(8,128)(2,1)S(1)} copy-done((bf16[16,640]{1,0:T(8,128)(2,1)S(1)}, bf16[16,640]{1,0:T(8,128)(2,1)}, u32[]{:S(2)}) %copy-start.2) | copy-done | bytes 20504
  4.9 57.9 %shard_map.59 = (bf16[2048,2048]{1,0:T(8,128)(2,1)S(1)}, f32[16,128]{1,0:T(8,128)S(1)}) custom-call(bf16[16,640]{1,0:T(8,128)(2,1)S(1)} %copy-done.2, bf16[640,640]{1,0:T(8,128)(2,1)S(1)} %copy-done.1, bf16[2048,640]{1,0:T(8,128)(2,1)S(1)} %copy-done, f32[1]{0:T(128)S(6)} %copy.10.scale_ref), custom_call_target="tpu_custom_call" | custom-call | tf_op jit(solution)/shard_map/pallas_call | solution.py:202
  62.8 3.4 %copy.8 = bf16[2048,2048]{1,0:T(8,128)(2,1)} copy(bf16[2048,2048]{1,0:T(8,128)(2,1)S(1)} %get-tuple-element.6) | data formatting | bytes 16777216
  66.2 0.6 copy.9
Async XLA Ops:
  1.3 1.7 %copy-start = (bf16[2048,640]{1,0:T(8,128)(2,1)S(1)}, bf16[2048,640]{1,0:T(8,128)(2,1)}, u32[]{:S(2)}) copy-start(bf16[2048,640]{1,0:T(8,128)(2,1)} %g_hbm.1) | copy-start | bytes 7864324
  3.0 1.1 %copy-start.1 = (bf16[640,640]{1,0:T(8,128)(2,1)S(1)}, bf16[640,640]{1,0:T(8,128)(2,1)}, u32[]{:S(2)}) copy-start(bf16[640,640]{1,0:T(8,128)(2,1)} %w_hbm.1) | copy-start | bytes 2457604
  4.2 0.7 %copy-start.2 = (bf16[16,640]{1,0:T(8,128)(2,1)S(1)}, bf16[16,640]{1,0:T(8,128)(2,1)}, u32[]{:S(2)}) copy-start(bf16[16,640]{1,0:T(8,128)(2,1)} %t_hbm.1) | copy-start | bytes 61444

commit v2 on v0

v2 whole, which is shorter than its diff:
```python
import jax
import jax.numpy as jnp
from jax import lax
from jax.experimental import pallas as pl
from jax.experimental.pallas import tpu as pltpu
from jax.sharding import PartitionSpec as P

MESH = pl.DeviceIdType.MESH
LOG2E = 1.4426950408889634
NEAR = (1, 3, 2)


def device_of(z, y, x, core):
    return ((z * 4 + y) * 4 + x) * 2 + core


def mod4(v):
    return lax.rem(v, 4)


def natural_order(v):
    row = lax.broadcasted_iota(jnp.int32, (16, 128), 0)
    lane = lax.broadcasted_iota(jnp.int32, (16, 128), 1)
    x, odd, r = lane // 32, lax.rem(lane // 16, 2), lax.rem(lane, 16)
    z, half = row // 4, lax.rem(row, 2) * 64

    def rows(pick):
        return jnp.concatenate([v[pick(i // 4, i % 4):pick(i // 4, i % 4) + 1] for i in range(16)], axis=0)

    out = jnp.take_along_axis(rows(lambda z, y: z * 2 + y // 2), half + x * 16 + r, axis=1)
    for at in range(4):
        part = jnp.take_along_axis(rows(lambda z, y: 8 + at * 2 + y // 2), half + z * 16 + r, axis=1)
        out = jnp.where((odd == 1) & (x == at), part, out)
    return out


def kernel(t_hbm, w_hbm, g_hbm, scale_ref, e_buf, maxt_buf, stat_own,
           t_buf, w_buf, g_buf, g_t, q_all, d_buf0, d_buf1, part_buf0, part_buf1, stat_in,
           load_sem, gs_sem, gr_sem, ss_sem, sr_sem):
    me = lax.axis_index("ga")
    core = lax.rem(me, 2)
    z, y, x = me // 32, mod4(me // 8), mod4(me // 2)
    partner = me + 1 - 2 * core
    first = x + core * (z - x)
    last = z + core * (x - z)

    def peer_first(k):
        f = mod4(first + k)
        return device_of(z + core * (f - z), y, f + core * (x - f), core)

    def peer_y(k):
        return device_of(z, mod4(y + k), x, core)

    def peer_last(k):
        f = mod4(last + k)
        return device_of(f + core * (z - f), y, x + core * (f - x), core)

    peers = {(n, k): f(k) for n, f in (("f", peer_first), ("y", peer_y), ("l", peer_last)) for k in (1, 2, 3)}

    loads = [pltpu.make_async_copy(src, dst, load_sem.at[i])
             for i, (src, dst) in enumerate(((t_hbm, t_buf), (w_hbm, w_buf), (g_hbm, g_buf)))]
    for load in loads:
        load.start()
    barrier = pltpu.get_barrier_semaphore()
    for to in (partner, *peers.values()):
        pl.semaphore_signal(barrier, inc=1, device_id=(to,), device_id_type=MESH)

    mult = jnp.exp(jnp.full((1, 128), scale_ref[0], jnp.float32))
    coef = mult * (LOG2E / 2)

    loads[0].wait()
    loads[1].wait()
    u = jnp.dot(t_buf[...], w_buf[...], preferred_element_type=jnp.float32)
    unit = u / jnp.sqrt(jnp.sum(u * u, axis=1, keepdims=True))
    q_all[core, last, y, first] = (unit * 2.0).astype(jnp.bfloat16)
    pl.semaphore_wait(barrier, 10)

    sends = []

    def send(ref, slot, to):
        copy = pltpu.make_async_remote_copy(ref, ref, gs_sem.at[slot], gr_sem.at[slot],
                                            device_id=(to,), device_id_type=MESH)
        copy.start()

    def recv(ref, slot):
        pltpu.make_async_remote_copy(ref, ref, gs_sem.at[slot], gr_sem.at[slot],
                                     device_id=(partner,), device_id_type=MESH).wait_recv()

    def line(c, k, j):
        at = last if c is core else first
        return q_all.at[c, mod4(at + 4 - k), mod4(y + 4 - j)]

    other = 1 - core

    def to_partner(k, j):
        send(line(core, k, j), 18 + k * 4 + j, partner)

    def from_partner(k):
        for j in range(4):
            recv(line(other, k, j), 18 + k * 4 + j)

    def to_last(j, k):
        send(line(core, 0, j), 6 + (k - 1) * 4 + j, peers["l", k])

    def from_last(k):
        for j in range(4):
            recv(line(core, k, j), 6 + (k - 1) * 4 + j)
            to_partner(k, j)

    def transpose(lo, hi):
        for n in range(lo, hi):
            g_t[:, n * 256:(n + 1) * 256] = g_buf[n * 256:(n + 1) * 256, :].T

    for k in NEAR:
        send(q_all.at[core, last, y, first], k - 1, peers["f", k])
    loads[2].wait()
    transpose(0, 4)
    for ref in (d_buf1, part_buf0, part_buf1):
        ref[...] = jnp.zeros_like(ref)
    for k in NEAR:
        recv(q_all.at[core, last, y, mod4(first + 4 - k)], k - 1)
    for k in NEAR:
        send(line(core, 0, 0), 2 + k, peers["y", k])
    for k in NEAR:
        to_last(0, k)
    to_partner(0, 0)
    transpose(4, 8)
    for j in NEAR:
        recv(line(core, 0, j), 2 + j)
        to_last(j, 1)
        to_last(j, 3)
        to_partner(0, j)
    for j in NEAR:
        to_last(j, 2)

    base = (me * 2048).astype(jnp.float32)
    lane = lax.broadcasted_iota(jnp.int32, (128, 128), 0).astype(jnp.float32) + base

    def plane_of(c, k):
        at = mod4((last if c is core else first) + 4 - k)
        return c, at, c * 4 + at

    def scores(plane, d_ref, n):
        c, at, _ = plane
        cols = slice(n * 512, (n + 1) * 512)
        d_ref[:, cols] = jnp.dot(q_all[c, at].reshape(256, 640), g_t[:, cols], preferred_element_type=jnp.float32)

    def softmax(plane, d_ref, part_ref, n):
        for j in range(n * 8, n * 8 + 8):
            r8 = pl.ds(j * 8, 8)
            to = pl.ds(pl.multiple_of(plane[2] * 256 + j * 8, 8), 8)
            d = [d_ref[r8, i * 128:(i + 1) * 128] for i in range(16)]
            top = d
            while len(top) > 1:
                top = [jnp.maximum(a, b) for a, b in zip(top[::2], top[1::2])]
            top = top[0]
            total = weighted = None
            for i in range(15, -1, -1):
                e = jnp.exp2((d[i] - top) * coef)
                e_buf[to, i * 128:(i + 1) * 128] = e
                total = e if total is None else total + e
                if i == 15:
                    weighted = total
                elif i > 0:
                    weighted = weighted + total
            part_ref[0, r8, :] = top
            part_ref[1, r8, :] = total
            part_ref[2, r8, :] = weighted

    def statistics(plane, part_ref, h):
        r128 = pl.ds(pl.multiple_of(plane[2] * 256 + h * 128, 128), 128)
        m_t, z_t, w_t = (part_ref[i, h * 128:(h + 1) * 128, :].T for i in range(3))
        m = jnp.max(m_t, axis=0, keepdims=True)
        scale = jnp.exp2((m_t - m) * coef)
        maxt_buf[r128, :] = m_t
        row = pl.ds(plane[2] * 2 + h, 1)
        stat_own[0, row, :] = m
        stat_own[1, row, :] = jnp.sum(z_t * scale, axis=0, keepdims=True)
        stat_own[2, row, :] = jnp.sum((z_t * lane + w_t * 128.0) * scale, axis=0, keepdims=True)

    def step(new, d_new, part_new, old, d_old, older, part_older):
        for n in range(4):
            if new is not None:
                scores(plane_of(*new), d_new, n)
            if n < 2:
                statistics(plane_of(*older), part_older, n)
            if old is not None:
                softmax(plane_of(*old), d_old, part_new, n)

    @pl.loop(0, 4)
    def _(i):
        k, before = (v + v // 2 - 2 * (v // 3) for v in (i, mod4(i + 3)))

        @pl.when(i == 1)
        def _():
            from_last(1)

        step((core, k), d_buf0, part_buf1, (other, before), d_buf1, (core, before), part_buf0)

        @pl.when(i == 1)
        def _():
            from_last(3)

        @pl.when(i == 2)
        def _():
            from_last(2)

        from_partner(k)
        step((other, k), d_buf1, part_buf0, (core, k), d_buf0, (other, before), part_buf1)

    step(None, None, part_buf1, (other, 2), d_buf1, (core, 2), part_buf0)
    step(None, None, None, None, None, (other, 2), part_buf1)

    def merge(parts):
        m = parts[0][0]
        for part in parts[1:]:
            m = jnp.maximum(m, part[0])
        total = rank = None
        for pm, pz, ps in parts:
            f = jnp.exp2((pm - m) * coef)
            total = pz * f if total is None else total + pz * f
            rank = ps * f if rank is None else rank + ps * f
        return m, total, rank

    for stage in range(4):
        if stage == 0:
            here, others, n = core, [(partner, 0)], 2
        else:
            here = (x, y, z)[stage - 1]
            others = [((device_of(z, y, mod4(x + k), core), device_of(z, mod4(y + k), x, core),
                        device_of(mod4(z + k), y, x, core))[stage - 1], k - 1) for k in NEAR]
            n = 4
        stat_in[stage, here] = stat_own[...]
        copies = []
        for to, k in others:
            copy = pltpu.make_async_remote_copy(
                stat_in.at[stage, here], stat_in.at[stage, here], ss_sem.at[stage, k], sr_sem.at[stage, k],
                device_id=(to,), device_id_type=MESH)
            copy.start()
            copies.append(copy)
            sends.append(copy)
        for copy in copies:
            copy.wait_recv()
        m, total, rank = merge([tuple(stat_in[stage, a, i] for i in range(3)) for a in range(n)])
        stat_own[0] = m
        stat_own[1] = total
        stat_own[2] = rank
    stat_own[2] = rank / (total * 262144.0)

    for copy in sends:
        copy.wait_send()
    for slot in range(34):
        ref = q_all.at[core, last, y, first] if slot < 3 else line(core, 0, 0)
        pltpu.make_async_remote_copy(ref, ref, gs_sem.at[slot], gr_sem.at[slot],
                                     device_id=(partner,), device_id_type=MESH).wait_send()


def scale_kernel(e_ref, maxt_ref, stat_ref, scale_ref, p_hbm, rank_hbm, p_buf, rank_buf, sem, rank_sem):
    coef = jnp.exp(jnp.full((1, 128), scale_ref[0], jnp.float32)) * (LOG2E / 2)
    rank_buf[...] = natural_order(stat_ref[2])
    rank = pltpu.make_async_copy(rank_buf, rank_hbm, rank_sem)
    rank.start()
    copies = [rank]
    for b in range(16):
        c, at, h = b // 8, (b // 2) % 4, b % 2
        m = stat_ref[0, b:b + 1, :]
        total = stat_ref[1, b:b + 1, :]
        factor = (jnp.exp2((maxt_ref[b * 128:(b + 1) * 128, :] - m) * coef) / total).T
        for line in range(2):
            for f in range(4):
                block = line * 4 + f
                r16 = slice(b * 128 + block * 16, b * 128 + block * 16 + 16)
                part = factor[block * 16:block * 16 + 16]
                for i in range(16):
                    p_buf[b, line, f, :, i * 128:(i + 1) * 128] = (e_ref[r16, i * 128:(i + 1) * 128] * part).astype(jnp.bfloat16)
            y = h * 2 + line
            to = p_hbm.at[at, y, :, 0] if c == 0 else p_hbm.at[:, y, at, 1]
            copy = pltpu.make_async_copy(p_buf.at[b, line], to, sem.at[b, line])
            copy.start()
            copies.append(copy)
    for copy in copies:
        copy.wait()


def solution(mesh):
    def per_device(text_states, text_proj, gallery, logit_scale):
        f32, bf16 = jnp.float32, jnp.bfloat16
        vmem = pl.BlockSpec(memory_space=pltpu.VMEM)
        smem = pl.BlockSpec(memory_space=pltpu.SMEM)
        e, maxt, stat = pl.pallas_call(
            kernel,
            out_shape=[pltpu.VMEM((2048, 2048), f32), pltpu.VMEM((2048, 128), f32), pltpu.VMEM((3, 16, 128), f32)],
            in_specs=[pl.BlockSpec(memory_space=pltpu.HBM)] * 3 + [smem],
            out_specs=[vmem] * 3,
            scratch_shapes=[
                pltpu.VMEM((16, 640), bf16),
                pltpu.VMEM((640, 640), bf16),
                pltpu.VMEM((2048, 640), bf16),
                pltpu.VMEM((640, 2048), bf16),
                pltpu.VMEM((2, 4, 4, 4, 16, 640), bf16),
                pltpu.VMEM((256, 2048), f32),
                pltpu.VMEM((256, 2048), f32),
                pltpu.VMEM((3, 256, 128), f32),
                pltpu.VMEM((3, 256, 128), f32),
                pltpu.VMEM((4, 4, 3, 16, 128), f32),
                pltpu.SemaphoreType.DMA((3,)),
                pltpu.SemaphoreType.DMA((34,)),
                pltpu.SemaphoreType.DMA((34,)),
                pltpu.SemaphoreType.DMA((4, 3)),
                pltpu.SemaphoreType.DMA((4, 3)),
            ],
            compiler_params=pltpu.CompilerParams(
                collective_id=0, has_side_effects=True, vmem_limit_bytes=36 * 2**20),
        )(*(pltpu.with_memory_space_constraint(v, pltpu.HBM) for v in (text_states, text_proj, gallery)), logit_scale)
        p, rank = pl.pallas_call(
            scale_kernel,
            out_shape=[jax.ShapeDtypeStruct((4, 4, 4, 2, 16, 2048), bf16), jax.ShapeDtypeStruct((16, 128), f32)],
            in_specs=[vmem] * 3 + [smem],
            out_specs=[pl.BlockSpec(memory_space=pltpu.HBM)] * 2,
            scratch_shapes=[
                pltpu.VMEM((16, 2, 4, 16, 2048), bf16),
                pltpu.VMEM((16, 128), f32),
                pltpu.SemaphoreType.DMA((16, 2)),
                pltpu.SemaphoreType.DMA,
            ],
            compiler_params=pltpu.CompilerParams(vmem_limit_bytes=36 * 2**20),
        )(e, maxt, stat, logit_scale)
        return p.reshape(2048, 2048), rank.reshape(2048)

    return jax.shard_map(per_device, mesh=mesh,
                         in_specs=(P("ga", None), P(None, None), P("ga", None), P(None)),
                         out_specs=(P(None, "ga"), P(None)), check_vma=False)
```

time: 320 us -> 48.2 us (0.15)
  blocking collectives: 189 us -> 0 us
  waiting for transfers between devices: 70.4 us -> 0 us
  Pallas kernels: 0 us -> 46.2 us
  other arithmetic: 20.1 us -> 0 us
  between operations: 14.7 us -> 1.29 us
  matrix products: 13 us -> 0 us
  local copies, waits for them, and re-layouts: 12.2 us -> 0 us
    psum x2 -> x0, blocking collectives: 126 us -> none  [the longest x1 63.8 us: per_device(): glob_sum = lax.psum(jnp.sum(exp_vals, axis=1), 'ga')]
    all_gather x1 -> x0, waiting for transfers between devices: 70.4 us -> none  [per_device(): all_queries = lax.all_gather(query_emb, 'ga', axis=0, tiled=True)]
    pmax x1 -> x0, blocking collectives: 62.3 us -> none  [per_device(): glob_max = lax.pmax(jnp.max(scores, axis=1), 'ga')]
    pallas_call x0 -> x2, Pallas kernels: none -> 46.2 us  [the longest x1 42.4 us: per_device(): pl.pallas_call(kernel, out_shape=[pltpu.VMEM((2048, 2048), f32), pltpu.VM...]
    reduce_sum x2 -> x0, other arithmetic: 19.4 us -> none  [the longest x1 10.9 us: per_device(): exp_rank = lax.psum(jnp.sum(prob_vals * positions, axis=1), 'ga')]
    dot_general x2 -> x0, matrix products: 13 us -> none  [the longest x1 11.3 us: per_device(): lax.dot_general(all_queries, gallery, (((1,), (1,)), ((), ())), preferred...]
    unnamed x3 -> x0, local copies, waits for them, and re-layouts: 12.2 us -> none
  transfers between devices with their start and end apart: 1 -> 0, of which waited for: 1 -> 0; matrix products, arithmetic and copies ran while one was open for 0% -> 0% of each run, Pallas kernels for 0% -> 0%
where the time goes in v2:
time: 48.2 us; the launch traced here: 47.4 us
  Pallas kernels  46.2 us (96%)
  between operations  1.29 us (3%)
    pallas_call x1, Pallas kernels, per_device(): pl.pallas_call(kernel, out_shape=[pltpu.VMEM((2048, 2048), f32), pltpu.VM...  42.4 us
    pallas_call x1, Pallas kernels, per_device(): pl.pallas_call(scale_kernel, out_shape=[jax.ShapeDtypeStruct((4, 4, 4, 2,...  3.74 us

profile of v2, /device:TPU:1, one launch (start us, length us, event | category | flops | bytes accessed | tf_op | source)
XLA Modules:
  0.0 47.4 jit_solution(8332199282973914409)
XLA Ops:
  1.3 42.4 %shard_map.59 = (f32[2048,2048]{1,0:T(8,128)S(1)}, f32[2048,128]{1,0:T(8,128)S(1)}, f32[3,16,128]{2,1,0:T(8,128)S(1)}) custom-call(bf16[16,640]{1,0:T(8,128)(2,1)} %t_hbm.1, bf16[640,640]{1,0:T(8,128)(2,1)} %w_hbm.1, bf16[2048,640]{1,0:T(8,128)(2,1)} %g_hbm.1, f32[1]{0:T(128)S(6)} %copy.6.scale_ref), custom_call_target="tpu_custom_call" | custom-call | tf_op jit(solution)/shard_map/pallas_call | solution.py:290
  43.7 3.7 %shard_map.60 = (bf16[4,4,4,2,16,2048]{5,4,3,2,1,0:T(8,128)(2,1)}, f32[16,128]{1,0:T(8,128)}) custom-call(f32[2048,2048]{1,0:T(8,128)S(1)} %get-tuple-element.7.e_ref, f32[2048,128]{1,0:T(8,128)S(1)} %get-tuple-element.8.maxt_ref, f32[3,16,128]{2,1,0:T(8,128)S(1)} %get-tuple-element.9.stat_ref, f32[1]{0:T(128)S(6)} %copy.6.scale_ref), custom_call_target="tpu_custom_call" | custom-call | tf_op jit(solution)/shard_map/pallas_call | solution.py:315
